TPU v7x, 32 devices: a whole 2x2x4 slice. The times are simulated.
32 devices in a mesh: img: 8 (over z, core), txt: 4 (over y, x).
Axes of the slice: x: 2, y: 2, z: 4, core: 2. Of those that a mesh axis runs over, the one named last changes fastest.
Arguments:
- teacher_img: bfloat16 [8192, 1280], P('img'), may hold values from -40 to 40
- teacher_txt: bfloat16 [4096, 1280], P('txt'), may hold values from -40 to 40
- student_img: bfloat16 [8192, 512], P('img'), may hold values from -40 to 40
- student_txt: bfloat16 [4096, 512], P('txt'), may hold values from -40 to 40
Outputs:
- loss: float32 [], replicated
- grad_img: float32 [8192, 512], P(('img', 'txt'))
- grad_txt: float32 [4096, 512], P(('txt', 'img'))
All inputs are finite; a program needn't handle non-finite values.
Results may differ from a plain program's by a relative error of at most 0.0033.
Values sent between devices are 32-bit elements; how exact they have to be, the bound alone decides.
A program may use at most 64 MiB of HBM per device.

v0:
```python
import functools
import math

import jax
import jax.numpy as jnp
from jax import lax
from jax.experimental import pallas as pl
from jax.experimental.pallas import tpu as pltpu
from jax.sharding import PartitionSpec as P

LANES = 128
LOG2E = math.log2(math.e)
LN2 = math.log(2.0)
MESH = pl.DeviceIdType.MESH
F32 = jnp.float32
NT = (((1,), (1,)), ((), ()))


def minor_of(n):
    return 1 << ((n.bit_length() - 1) // 2)


def kernel(
    img_n, txt_n,
    timg_hbm, ttxt_hbm, simg_hbm, stxt_hbm,
    loss_ref, gimg_ref, gtxt_ref,
    timg, ttxt, simg, stxt, t2, s2, row_at, cstat, rslot, cslot, delta, deltat,
    gi, g1a, g1b, g2a, g2b, gt, xr, rr, rl, lrow, lcol,
    in_sem, rs_send, rs_recv, cs_send, cs_recv, a1_send, a1_recv, b1_send, b1_recv,
    a2_send, a2_recv, b2_send, b2_recv, x_send, x_recv,
    z_send, z_recv, l1_send, l1_recv, l2_send, l2_recv,
):
    rows, wide = timg.shape
    cols, deep = stxt.shape
    strips = rows // LANES
    pieces = cols // LANES
    mi = lax.axis_index("img")
    mt = lax.axis_index("txt")
    levels = img_n // 2
    mz = mi // 2
    mc = lax.rem(mi, 2)
    scale_t = 3.0 / math.sqrt(wide) * LOG2E
    scale_s = 3.0 / math.sqrt(deep) * LOG2E
    scale_g = 3.0 / math.sqrt(deep)

    loads = [
        pltpu.make_async_copy(src, dst, in_sem.at[k])
        for k, (src, dst) in enumerate(
            ((timg_hbm, timg), (ttxt_hbm, ttxt), (simg_hbm, simg), (stxt_hbm, stxt))
        )
    ]
    for load in loads:
        load.start()

    barrier = pltpu.get_barrier_semaphore()
    txt_peers = [lax.rem(mt + d, txt_n) for d in range(1, txt_n)]
    img_peers = [lax.rem(mi + d, img_n) for d in range(1, img_n)]
    for p in txt_peers:
        pl.semaphore_signal(barrier, inc=1, device_id=(mi, p), device_id_type=MESH)
    for p in img_peers:
        pl.semaphore_signal(barrier, inc=1, device_id=(p, mt), device_id_type=MESH)

    def to_txt(src, dst, send, recv, p):
        return pltpu.make_async_remote_copy(
            src_ref=src, dst_ref=dst, send_sem=send, recv_sem=recv,
            device_id=(mi, p), device_id_type=MESH,
        )

    def to_img(src, dst, send, recv, p):
        return pltpu.make_async_remote_copy(
            src_ref=src, dst_ref=dst, send_sem=send, recv_sem=recv,
            device_id=(p, mt), device_id_type=MESH,
        )

    lane = lax.broadcasted_iota(jnp.int32, (8, LANES), 1)

    chunk = min(2 * LANES, cols)
    stat_out = []

    def product(left, right, out, factor, slot):
        def one(j, c):
            at = pl.ds(pl.multiple_of(j * chunk, chunk), chunk)
            tile = factor * lax.dot_general(
                left[...], right[at, :], NT, preferred_element_type=F32
            )
            out[:, at] = tile
            cstat[slot, 0:1, at] = jnp.max(tile, axis=0, keepdims=True)
            return c

        lax.fori_loop(0, cols // chunk, one, 0)

    def masses(out, slot):
        def group(g, mass):
            here = pl.ds(pl.multiple_of(g * 8, 8), 8)
            x = out[here, :]
            peak = jnp.max(x, axis=1, keepdims=True)
            row = jnp.sum(jnp.exp2(x - peak), axis=1, keepdims=True)
            row_at[slot, here, :] = jnp.where(lane == 0, peak, row)
            return mass + jnp.exp2(x - cstat[slot, 0:1, :])

        mass = lax.fori_loop(0, rows // 8, group, jnp.zeros((8, cols), F32), unroll=8)
        tops = cstat[slot, 0:1, :]
        sums = jnp.sum(mass, axis=0, keepdims=True)
        for k in range(pieces):
            at = slice(k * LANES, (k + 1) * LANES)
            cslot[slot, mi, 0, k : k + 1, :] = tops[:, at]
            cslot[slot, mi, 1, k : k + 1, :] = sums[:, at]
        for k in range(strips):
            turned = row_at[slot, k * LANES : (k + 1) * LANES, :].T
            rslot[slot, mt, 0, k : k + 1, :] = turned[0:1, :]
            rslot[slot, mt, 1, k : k + 1, :] = turned[1:2, :]
        if slot == 0:
            pl.semaphore_wait(barrier, txt_n - 1 + img_n - 1)
        copies = [
            to_img(
                cslot.at[slot, mi], cslot.at[slot, mi],
                cs_send.at[slot, d], cs_recv.at[slot, mi], p,
            )
            for d, p in reversed(list(enumerate(img_peers)))
        ] + [
            to_txt(
                rslot.at[slot, mt], rslot.at[slot, mt],
                rs_send.at[slot, d], rs_recv.at[slot, mt], p,
            )
            for d, p in enumerate(txt_peers)
        ]
        for copy in copies:
            copy.start()
        stat_out.extend(copies)

    loads[0].wait()
    loads[1].wait()
    product(timg, ttxt, t2, scale_t, 0)
    masses(t2, 0)
    loads[2].wait()
    loads[3].wait()
    product(simg, stxt, s2, scale_s, 1)
    masses(s2, 1)

    def joined(slot, n):
        peaks = [slot[k, 0] for k in range(n)]
        top = functools.reduce(jnp.maximum, peaks)
        mass = functools.reduce(
            jnp.add, [slot[k, 1] * jnp.exp2(peaks[k] - top) for k in range(n)]
        )
        return top + jnp.log(mass) * LOG2E

    pad = jnp.zeros((LANES - 8, LANES), F32)

    def gathered(slot):
        for d, p in enumerate(txt_peers):
            to_txt(
                rslot.at[slot, p], rslot.at[slot, p],
                rs_send.at[slot, d], rs_recv.at[slot, p], p,
            ).wait_recv()
        row = joined(rslot.at[slot], txt_n)
        for k in range(strips):
            row_at[slot, k * LANES : (k + 1) * LANES, :] = jnp.concatenate(
                [jnp.broadcast_to(row[k : k + 1], (8, LANES)), pad], axis=0
            ).T
        for d, p in enumerate(img_peers):
            to_img(
                cslot.at[slot, p], cslot.at[slot, p],
                cs_send.at[slot, d], cs_recv.at[slot, p], p,
            ).wait_recv()
        col = joined(cslot.at[slot], img_n)
        for k in range(pieces):
            cstat[slot, 0:1, k * LANES : (k + 1) * LANES] = col[k : k + 1]
        return row, col

    row_t, col_t = gathered(0)

    def teacher_group(g, acc):
        here = pl.ds(pl.multiple_of(g * 8, 8), 8)
        tg = t2[here, :]
        gap = tg - s2[here, :]
        p_row = jnp.exp2(tg - row_at[0, here, 0:1])
        p_col = jnp.exp2(tg - cstat[0, 0:1, :])
        t2[here, :] = p_row + p_col
        return acc + (
            p_row * (1.0 / (rows * img_n)) + p_col * (1.0 / (cols * txt_n))
        ) * gap

    total = lax.fori_loop(0, rows // 8, teacher_group, jnp.zeros((8, cols), F32), unroll=4)
    row_s, col_s = gathered(1)

    def delta_strip(start):
        def group(g, c):
            here = pl.ds(pl.multiple_of(start + g * 16, 16), 16)
            sg = s2[here, :]
            d = (
                jnp.exp2(sg - row_at[1, here, 0:1])
                + jnp.exp2(sg - cstat[1, 0:1, :])
                - t2[here, :]
            )
            delta[here, :] = (8.0 * d).astype(jnp.bfloat16)
            return c

        lax.fori_loop(0, LANES // 16, group, 0, unroll=4)
        at = pl.ds(pl.multiple_of(start, LANES), LANES)
        deltat[:, at] = delta[at, :].T

    per = rows // txt_n
    cper = cols // img_n

    def rows_of(p):
        return pl.ds(pl.multiple_of(p * per, per), per)

    def cols_of(o):
        return pl.ds(pl.multiple_of(o * cper, cper), cper)

    fine = per % LANES == 0
    if not fine:
        lax.fori_loop(0, strips, lambda k, c: (delta_strip(k * LANES), c)[1], 0)

    gi_out = []
    minor = minor_of(txt_n)
    major = txt_n // minor
    my, mx = mt // minor, lax.rem(mt, minor)
    part = per // 2

    def block(y, x, w):
        return pl.ds(pl.multiple_of((y * minor + x) * per + w * part, part), part)

    ys = [lax.rem(my + d, major) for d in range(1, major)]
    xs = [lax.rem(mx + d, minor) for d in range(1, minor)]
    for y in [*ys, my]:
        for x in [*xs, mx]:
            p = y * minor + x
            if fine:
                lax.fori_loop(
                    0, per // LANES,
                    lambda k, c, p=p: (delta_strip(p * per + k * LANES), c)[1], 0,
                )
            gi[rows_of(p), :] = scale_g * jnp.dot(
                delta[rows_of(p), :], stxt[...], preferred_element_type=F32
            )
            copies = []
            if x is not mx:
                copies.append(to_txt(
                    gi.at[block(y, x, 0), :], g1a.at[mx, y],
                    a1_send.at[x, y], a1_recv.at[mx, y], my * minor + x,
                ))
            if y is not my:
                copies.append(to_txt(
                    gi.at[block(y, x, 1), :], g1b.at[my, x],
                    b1_send.at[y, x], b1_recv.at[my, x], y * minor + mx,
                ))
            for copy in copies:
                copy.start()
            gi_out.extend(copies)

    def take_a(y):
        for x in xs:
            to_txt(
                g1a.at[x, y], g1a.at[x, y], a1_send.at[x, y], a1_recv.at[x, y],
                my * minor + x,
            ).wait_recv()
            gi[block(y, mx, 0), :] = gi[block(y, mx, 0), :] + g1a[x, y]

    def take_b(x):
        for y in ys:
            to_txt(
                g1b.at[y, x], g1b.at[y, x], b1_send.at[y, x], b1_recv.at[y, x],
                y * minor + mx,
            ).wait_recv()
            gi[block(my, x, 1), :] = gi[block(my, x, 1), :] + g1b[y, x]

    def second_leg():
        for y in ys:
            take_a(y)
            copy = to_txt(
                gi.at[block(y, mx, 0), :], g2a.at[my], a2_send.at[y], a2_recv.at[my],
                y * minor + mx,
            )
            copy.start()
            gi_out.append(copy)
        for x in xs:
            take_b(x)
            copy = to_txt(
                gi.at[block(my, x, 1), :], g2b.at[mx], b2_send.at[x], b2_recv.at[mx],
                my * minor + x,
            )
            copy.start()
            gi_out.append(copy)

    def text_term(o):
        gt[cols_of(o), :] = scale_g * jnp.dot(
            deltat[cols_of(o), :], simg[...], preferred_element_type=F32
        )

    mate = mi + 1 - 2 * mc
    high = (2 * mz) // levels
    ends_in = [k // 2 if k % 2 else levels - 1 - k // 2 for k in range(levels)]
    order = [e + high * (levels - 1 - 2 * e) for e in ends_in]
    x_out = []
    for d, b in enumerate(order):
        o = 2 * b + 1 - mc
        text_term(o)
        copy = to_img(gt.at[cols_of(o), :], xr.at[b], x_send.at[b], x_recv.at[b], mate)
        copy.start()
        x_out.append(copy)
    half = cper // 2

    def hop(b, h, way):
        slot = (rl, rr)[way].at[b, pl.ds(h * half, half), :]
        at = pl.ds(pl.multiple_of((2 * b + mc) * cper + h * half, half), half)
        return at, slot, to_img(
            gt.at[at, :], slot, z_send.at[way, b, h], z_recv.at[way, b, h],
            mi + (2 if way else -2),
        )

    def onward(b, h, way):
        at, slot, copy = hop(b, h, way)

        @pl.when(mz > 0 if way else mz < levels - 1)
        def _():
            copy.wait_recv()
            gt[at, :] = gt[at, :] + slot[...]

        copy.start()

    for d, b in enumerate(order):
        if d == levels // 2:
            second_leg()
        text_term(2 * b + mc)
        to_img(xr.at[b], xr.at[b], x_send.at[b], x_recv.at[b], mate).wait_recv()
        gt[cols_of(2 * b + mc), :] = gt[cols_of(2 * b + mc), :] + xr[b]

        @pl.when(b > mz)
        def _(b=b):
            onward(b, 0, 1)
            onward(b, 1, 1)

        @pl.when(b < mz)
        def _(b=b):
            onward(b, 0, 0)
            onward(b, 1, 0)

    mine = (
        jnp.sum(total)
        + jnp.sum(row_s - row_t) * (1.0 / (rows * img_n * txt_n))
        + jnp.sum(col_s - col_t) * (1.0 / (cols * txt_n * img_n))
    )
    lrow[mt] = jnp.full((8, LANES), mine, F32)
    l1_out = [
        to_txt(lrow.at[mt], lrow.at[mt], l1_send.at[d], l1_recv.at[mt], p)
        for d, p in enumerate(txt_peers)
    ]
    for copy in l1_out:
        copy.start()
    for d, p in enumerate(txt_peers):
        to_txt(lrow.at[p], lrow.at[p], l1_send.at[d], l1_recv.at[p], p).wait_recv()
    lcol[mi] = functools.reduce(jnp.add, [lrow[k] for k in range(txt_n)])
    l2_out = [
        to_img(lcol.at[mi], lcol.at[mi], l2_send.at[d], l2_recv.at[mi], p)
        for d, p in enumerate(img_peers)
    ]
    for copy in l2_out:
        copy.start()
    for d, p in enumerate(img_peers):
        to_img(lcol.at[p], lcol.at[p], l2_send.at[d], l2_recv.at[p], p).wait_recv()
    loss_ref[...] = (0.5 * LN2) * functools.reduce(jnp.add, [lcol[k] for k in range(img_n)])

    take_a(my)
    take_b(mx)
    for y in ys:
        to_txt(
            g2a.at[y], g2a.at[y], a2_send.at[y], a2_recv.at[y], y * minor + mx
        ).wait_recv()
        gi[block(my, mx, 0), :] = gi[block(my, mx, 0), :] + g2a[y]
    for x in xs:
        to_txt(
            g2b.at[x], g2b.at[x], b2_send.at[x], b2_recv.at[x], my * minor + x
        ).wait_recv()
        gi[block(my, mx, 1), :] = gi[block(my, mx, 1), :] + g2b[x]
    gimg_ref[...] = gi[rows_of(mt), :]
    for way in (0, 1):
        @pl.when(mz > 0 if way else mz < levels - 1)
        def _(way=way):
            for h in range(2):
                at, slot, copy = hop(mz, h, way)
                copy.wait_recv()
                gt[at, :] = gt[at, :] + slot[...]

    gtxt_ref[...] = gt[cols_of(mi), :]
    for b in order:
        @pl.when(b > mz)
        def _(b=b):
            for h in range(2):
                hop(b, h, 1)[2].wait_send()

        @pl.when(b < mz)
        def _(b=b):
            for h in range(2):
                hop(b, h, 0)[2].wait_send()

    for copy in [*stat_out, *gi_out, *x_out, *l1_out, *l2_out]:
        copy.wait_send()


def hand_over(loss, gimg, gtxt, loss_out, gimg_out, gtxt_out):
    loss_out[0, 0] = loss[0, 0]
    gimg_out[...] = gimg[...]
    gtxt_out[...] = gtxt[...]


def body(img_n, txt_n, teacher_img, teacher_txt, student_img, student_txt):
    rows, wide = teacher_img.shape
    cols, deep = student_txt.shape
    levels = img_n // 2
    vmem = pltpu.VMEM
    minor = minor_of(txt_n)
    major = txt_n // minor
    part = rows // txt_n // 2
    dma = pltpu.SemaphoreType.DMA
    bf16 = jnp.bfloat16
    loss, grad_img, grad_txt = pl.pallas_call(
        functools.partial(kernel, img_n, txt_n),
        out_shape=(
            jax.ShapeDtypeStruct((8, LANES), F32),
            jax.ShapeDtypeStruct((rows // txt_n, deep), F32),
            jax.ShapeDtypeStruct((cols // img_n, deep), F32),
        ),
        in_specs=[pl.BlockSpec(memory_space=pltpu.HBM)] * 4,
        out_specs=tuple(pl.BlockSpec(memory_space=vmem) for _ in range(3)),
        scratch_shapes=[
            vmem((rows, wide), bf16), vmem((cols, wide), bf16),
            vmem((rows, deep), bf16), vmem((cols, deep), bf16),
            vmem((rows, cols), F32), vmem((rows, cols), F32),
            vmem((2, rows, LANES), F32), vmem((2, 8, cols), F32),
            vmem((2, txt_n, 2, rows // LANES, LANES), F32),
            vmem((2, img_n, 2, cols // LANES, LANES), F32),
            vmem((rows, cols), bf16), vmem((cols, rows), bf16),
            vmem((rows, deep), F32), vmem((minor, major, part, deep), F32),
            vmem((major, minor, part, deep), F32),
            vmem((major, part, deep), F32), vmem((minor, part, deep), F32),
            vmem((cols, deep), F32), vmem((levels, cols // img_n, deep), F32),
            vmem((levels, cols // img_n, deep), F32), vmem((levels, cols // img_n, deep), F32),
            vmem((txt_n, 8, LANES), F32), vmem((img_n, 8, LANES), F32),
            dma((4,)),
            dma((2, txt_n)), dma((2, txt_n)), dma((2, img_n)), dma((2, img_n)),
            dma((minor, major)), dma((minor, major)), dma((major, minor)), dma((major, minor)),
            dma((major,)), dma((major,)), dma((minor,)), dma((minor,)), dma((levels,)), dma((levels,)),
            dma((2, levels, 2)), dma((2, levels, 2)),
            dma((txt_n,)), dma((txt_n,)), dma((img_n,)), dma((img_n,)),
        ],
        compiler_params=pltpu.CompilerParams(
            collective_id=0, has_side_effects=True, vmem_limit_bytes=60 * 1024 * 1024
        ),
    )(teacher_img, teacher_txt, student_img, student_txt)
    loss, grad_img, grad_txt = pl.pallas_call(
        hand_over,
        out_shape=(
            jax.ShapeDtypeStruct((1, 1), F32),
            jax.ShapeDtypeStruct(grad_img.shape, F32),
            jax.ShapeDtypeStruct(grad_txt.shape, F32),
        ),
        in_specs=[pl.BlockSpec(memory_space=vmem)] * 3,
        out_specs=(
            pl.BlockSpec(memory_space=pltpu.SMEM),
            pl.BlockSpec(memory_space=vmem), pl.BlockSpec(memory_space=vmem),
        ),
    )(loss, grad_img, grad_txt)
    return loss.reshape(()), grad_img, grad_txt


def solution(mesh):
    placed = (P("img", None), P("txt", None), P("img", None), P("txt", None))
    return jax.shard_map(
        functools.partial(body, mesh.shape["img"], mesh.shape["txt"]),
        mesh=mesh,
        in_specs=placed,
        out_specs=(P(), P(("img", "txt"), None), P(("txt", "img"), None)),
        check_vma=False,
    )
```

profile of v0, /device:TPU:0, one launch (start us, length us, event | category | flops | bytes accessed | tf_op | source)
XLA Modules:
  0.0 57.0 jit_solution(9698241641140464591)
XLA Ops:
  0.6 54.3 %shard_map.67 = (f32[8,128]{1,0:T(8,128)}, f32[256,512]{1,0:T(8,128)}, f32[128,512]{1,0:T(8,128)}) custom-call(bf16[1024,1280]{1,0:T(8,128)(2,1)} %timg_hbm.1, bf16[1024,1280]{1,0:T(8,128)(2,1)} %ttxt_hbm.1, bf16[1024,512]{1,0:T(8,128)(2,1)} %simg_hbm.1, bf16[1024,512]{1,0:T(8,128)(2,1)} %stxt_hbm.1), custom_call_target="tpu_custom_call" | custom-call | tf_op jit(solution)/shard_map/pallas_call | solution.py:418
  55.0 2.0 %shard_map.68 = (f32[1,1]{1,0:T(1,128)}, f32[256,512]{1,0:T(8,128)}, f32[128,512]{1,0:T(8,128)}) custom-call(f32[8,128]{1,0:T(8,128)} %get-tuple-element.9.loss, f32[256,512]{1,0:T(8,128)} %get-tuple-element.10.gimg, f32[128,512]{1,0:T(8,128)} %get-tuple-element.11.gtxt), custom_call_target="tpu_custom_call" | custom-call | tf_op jit(solution)/shard_map/pallas_call | solution.py:452
where the time goes:
time: 57.1 us; the launch traced here: 57 us
  Pallas kernels  56.4 us (99%)
  between operations  0.64 us (1%)
    pallas_call x1, Pallas kernels, body(): pl.pallas_call(functools.partial(kernel, img_n, txt_n), out_shape=(jax.Sh...  54.3 us
    pallas_call x1, Pallas kernels, body(): pl.pallas_call(hand_over, out_shape=(jax.ShapeDtypeStruct((1, 1), F32), j...  2.03 us

commit v1 on v0

v1 whole, which is shorter than its diff:
```python
import functools
import math

import jax
import jax.numpy as jnp
from jax import lax
from jax.experimental import pallas as pl
from jax.experimental.pallas import tpu as pltpu
from jax.sharding import PartitionSpec as P

LANES = 128
LOG2E = math.log2(math.e)
LN2 = math.log(2.0)
MESH = pl.DeviceIdType.MESH
F32 = jnp.float32
NT = (((1,), (1,)), ((), ()))


def minor_of(n):
    return 1 << ((n.bit_length() - 1) // 2)


def kernel(
    img_n, txt_n,
    timg_hbm, ttxt_hbm, simg_hbm, stxt_hbm,
    loss_ref, gimg_ref, gtxt_ref,
    timg, ttxt, simg, stxt, t2, s2, q, row_at, cstat, rslot, cslot, delta, deltat,
    gi, g1a, g1b, g2a, g2b, gt, xr, zr, lrow, lcol,
    in_sem, rs_send, rs_recv, cs_send, cs_recv, a1_send, a1_recv, b1_send, b1_recv,
    a2_send, a2_recv, b2_send, b2_recv, x_send, x_recv,
    z_send, z_recv, l1_send, l1_recv, l2_send, l2_recv,
):
    rows, wide = timg.shape
    cols, deep = stxt.shape
    strips = rows // LANES
    pieces = cols // LANES
    mi = lax.axis_index("img")
    mt = lax.axis_index("txt")
    levels = img_n // 2
    mz = mi // 2
    mc = lax.rem(mi, 2)
    scale_t = 3.0 / math.sqrt(wide) * LOG2E
    scale_s = 3.0 / math.sqrt(deep) * LOG2E
    scale_g = 3.0 / math.sqrt(deep)

    loads = [
        pltpu.make_async_copy(src, dst, in_sem.at[k])
        for k, (src, dst) in enumerate(
            ((simg_hbm, simg), (stxt_hbm, stxt), (timg_hbm, timg), (ttxt_hbm, ttxt))
        )
    ]
    for load in loads:
        load.start()

    barrier = pltpu.get_barrier_semaphore()
    txt_peers = [lax.rem(mt + d, txt_n) for d in range(1, txt_n)]
    img_peers = [lax.rem(mi + d, img_n) for d in range(1, img_n)]
    for p in txt_peers:
        pl.semaphore_signal(barrier, inc=1, device_id=(mi, p), device_id_type=MESH)
    for p in img_peers:
        pl.semaphore_signal(barrier, inc=1, device_id=(p, mt), device_id_type=MESH)

    def to_txt(src, dst, send, recv, p):
        return pltpu.make_async_remote_copy(
            src_ref=src, dst_ref=dst, send_sem=send, recv_sem=recv,
            device_id=(mi, p), device_id_type=MESH,
        )

    def to_img(src, dst, send, recv, p):
        return pltpu.make_async_remote_copy(
            src_ref=src, dst_ref=dst, send_sem=send, recv_sem=recv,
            device_id=(p, mt), device_id_type=MESH,
        )

    lane = lax.broadcasted_iota(jnp.int32, (8, LANES), 1)

    chunk = min(2 * LANES, cols)
    stat_out = []

    def product(left, right, out, factor, slot):
        def one(j, c):
            at = pl.ds(pl.multiple_of(j * chunk, chunk), chunk)
            tile = factor * lax.dot_general(
                left[...], right[at, :], NT, preferred_element_type=F32
            )
            out[:, at] = tile
            cstat[slot, 0:1, at] = jnp.max(tile, axis=0, keepdims=True)
            return c

        lax.fori_loop(0, cols // chunk, one, 0)

    def masses(out, slot):
        def group(g, mass):
            here = pl.ds(pl.multiple_of(g * 8, 8), 8)
            x = out[here, :]
            peak = jnp.max(x, axis=1, keepdims=True)
            row = jnp.sum(jnp.exp2(x - peak), axis=1, keepdims=True)
            row_at[slot, here, :] = jnp.where(lane == 0, peak, row)
            return mass + jnp.exp2(x - cstat[slot, 0:1, :])

        mass = lax.fori_loop(0, rows // 8, group, jnp.zeros((8, cols), F32), unroll=8)
        tops = cstat[slot, 0:1, :]
        sums = jnp.sum(mass, axis=0, keepdims=True)
        for k in range(pieces):
            at = slice(k * LANES, (k + 1) * LANES)
            cslot[slot, mi, 0, k : k + 1, :] = tops[:, at]
            cslot[slot, mi, 1, k : k + 1, :] = sums[:, at]
        for k in range(strips):
            turned = row_at[slot, k * LANES : (k + 1) * LANES, :].T
            rslot[slot, mt, 0, k : k + 1, :] = turned[0:1, :]
            rslot[slot, mt, 1, k : k + 1, :] = turned[1:2, :]
        if slot == 1:
            pl.semaphore_wait(barrier, txt_n - 1 + img_n - 1)
        copies = [
            to_img(
                cslot.at[slot, mi], cslot.at[slot, mi],
                cs_send.at[slot, d], cs_recv.at[slot, mi], p,
            )
            for d, p in reversed(list(enumerate(img_peers)))
        ] + [
            to_txt(
                rslot.at[slot, mt], rslot.at[slot, mt],
                rs_send.at[slot, d], rs_recv.at[slot, mt], p,
            )
            for d, p in enumerate(txt_peers)
        ]
        for copy in copies:
            copy.start()
        stat_out.extend(copies)

    loads[0].wait()
    loads[1].wait()
    product(simg, stxt, s2, scale_s, 1)
    masses(s2, 1)
    loads[2].wait()
    loads[3].wait()
    product(timg, ttxt, t2, scale_t, 0)
    masses(t2, 0)

    def joined(slot, n):
        peaks = [slot[k, 0] for k in range(n)]
        top = functools.reduce(jnp.maximum, peaks)
        mass = functools.reduce(
            jnp.add, [slot[k, 1] * jnp.exp2(peaks[k] - top) for k in range(n)]
        )
        return top + jnp.log(mass) * LOG2E

    def gathered(slot):
        for d, p in enumerate(txt_peers):
            to_txt(
                rslot.at[slot, p], rslot.at[slot, p],
                rs_send.at[slot, d], rs_recv.at[slot, p], p,
            ).wait_recv()
        row = joined(rslot.at[slot], txt_n)
        for k in range(strips):
            row_at[slot, k * LANES : (k + 1) * LANES, :] = jnp.broadcast_to(
                row[k : k + 1], (LANES, LANES)
            ).T
        for d, p in enumerate(img_peers):
            to_img(
                cslot.at[slot, p], cslot.at[slot, p],
                cs_send.at[slot, d], cs_recv.at[slot, p], p,
            ).wait_recv()
        col = joined(cslot.at[slot], img_n)
        for k in range(pieces):
            cstat[slot, 0:1, k * LANES : (k + 1) * LANES] = col[k : k + 1]
        return row, col

    def spread(slot, here):
        return jnp.concatenate([row_at[slot, here, :]] * pieces, axis=1)

    row_s, col_s = gathered(1)

    def student_group(g, c):
        here = pl.ds(pl.multiple_of(g * 8, 8), 8)
        sg = s2[here, :]
        q[here, :] = jnp.exp2(sg - spread(1, here)) + jnp.exp2(sg - cstat[1, 0:1, :])
        return c

    lax.fori_loop(0, rows // 8, student_group, 0, unroll=8)
    row_t, col_t = gathered(0)

    per = rows // txt_n
    cper = cols // img_n
    wide_c = 2 * cper
    half = cper // 2
    mate = mi + 1 - 2 * mc
    high = (2 * mz) // levels
    zp = mz + high * (levels - 1 - 2 * mz)

    def real(b):
        return b + high * (levels - 1 - 2 * b)

    def rows_of(p):
        return pl.ds(pl.multiple_of(p * per, per), per)

    def cols_of(o):
        return pl.ds(pl.multiple_of(o * cper, cper), cper)

    def delta_block(b):
        first = pl.multiple_of(b * wide_c, LANES)
        group = 4 if strips % 4 == 0 else 1

        def some(g, c):
            for k in range(group):
                at = pl.ds(pl.multiple_of((g * group + k) * LANES, LANES), LANES)
                r = row_at[0, at, :]
                for n in range(wide_c // LANES):
                    cs = pl.ds(pl.multiple_of(first + n * LANES, LANES), LANES)
                    tg = t2[at, cs]
                    d = q[at, cs] - jnp.exp2(tg - r) - jnp.exp2(tg - cstat[0, 0:1, cs])
                    d = (8.0 * d).astype(jnp.bfloat16)
                    delta[at, cs] = d
                    deltat[cs, at] = d.T
            return c

        lax.fori_loop(0, strips // group, some, 0)

    x_out = []

    def text_pair(b):
        pair = pl.ds(pl.multiple_of(b * wide_c, wide_c), wide_c)
        gt[pair, :] = scale_g * jnp.dot(
            deltat[pair, :], simg[...], preferred_element_type=F32
        )
        o = 2 * b + 1 - mc
        copy = to_img(gt.at[cols_of(o), :], xr.at[b], x_send.at[b], x_recv.at[b], mate)
        copy.start()
        x_out.append(copy)

    def hop(b, h, way):
        at = pl.ds(pl.multiple_of((2 * b + mc) * cper + h * half, half), half)
        slot = zr.at[way, b, pl.ds(h * half, half), :]
        return at, slot, to_img(
            gt.at[at, :], slot, z_send.at[way, b, h], z_recv.at[way, b, h],
            mi + 4 * way - 2,
        )

    def merge_mate(b):
        to_img(xr.at[b], xr.at[b], x_send.at[b], x_recv.at[b], mate).wait_recv()
        at = cols_of(2 * b + mc)
        gt[at, :] = gt[at, :] + xr[b]

    def launch(bp):
        @pl.when(jnp.logical_and(zp == 0, bp > 0))
        def _():
            for h in range(2):
                hop(real(bp), h, 1 - high)[2].start()

    far = list(reversed(range(levels)))
    lag = 2
    for n, bp in enumerate(far):
        delta_block(real(bp))
        text_pair(real(bp))
        if n >= lag:
            merge_mate(real(far[n - lag]))
            launch(far[n - lag])

    gi_out = []
    minor = minor_of(txt_n)
    major = txt_n // minor
    my, mx = mt // minor, lax.rem(mt, minor)
    part = per // 2

    def block(y, x, w):
        return pl.ds(pl.multiple_of((y * minor + x) * per + w * part, part), part)

    ys = [lax.rem(my + d, major) for d in range(1, major)]
    xs = [lax.rem(mx + d, minor) for d in range(1, minor)]

    def image_term(y, x):
        p = y * minor + x
        gi[rows_of(p), :] = scale_g * jnp.dot(
            delta[rows_of(p), :], stxt[...], preferred_element_type=F32
        )

    def begin(copies):
        for copy in copies:
            copy.start()
        gi_out.extend(copies)

    def image_a(y, x):
        return to_txt(
            gi.at[block(y, x, 0), :], g1a.at[mx, y],
            a1_send.at[x, y], a1_recv.at[mx, y], my * minor + x,
        )

    def image_b(y, x):
        return to_txt(
            gi.at[block(y, x, 1), :], g1b.at[my, x],
            b1_send.at[y, x], b1_recv.at[my, x], y * minor + mx,
        )

    for y in ys:
        for x in xs:
            image_term(y, x)
            begin([image_a(y, x), image_b(y, x)])
    for bp in far[max(0, levels - lag) :]:
        merge_mate(real(bp))
        if bp > 1:
            launch(bp)
    for y in ys:
        image_term(y, mx)
    for x in xs:
        image_term(my, x)
    image_term(my, mx)

    def teacher_group(g, acc):
        here = pl.ds(pl.multiple_of(g * 8, 8), 8)
        tg = t2[here, :]
        gap = tg - s2[here, :]
        p_row = jnp.exp2(tg - spread(0, here))
        p_col = jnp.exp2(tg - cstat[0, 0:1, :])
        return acc + (
            p_row * (1.0 / (rows * img_n)) + p_col * (1.0 / (cols * txt_n))
        ) * gap

    total = lax.fori_loop(0, rows // 8, teacher_group, jnp.zeros((8, cols), F32), unroll=4)
    mine = (
        jnp.sum(total)
        + jnp.sum(row_s - row_t) * (1.0 / (rows * img_n * txt_n))
        + jnp.sum(col_s - col_t) * (1.0 / (cols * txt_n * img_n))
    )
    lrow[mt] = jnp.full((8, LANES), mine, F32)
    l1_out = [
        to_txt(lrow.at[mt], lrow.at[mt], l1_send.at[d], l1_recv.at[mt], p)
        for d, p in enumerate(txt_peers)
    ]
    for copy in l1_out:
        copy.start()
    for x in xs:
        begin([image_a(my, x)])
    for y in ys:
        begin([image_b(y, mx)])

    def take_a(y):
        for x in xs:
            to_txt(
                g1a.at[x, y], g1a.at[x, y], a1_send.at[x, y], a1_recv.at[x, y],
                my * minor + x,
            ).wait_recv()
            gi[block(y, mx, 0), :] = gi[block(y, mx, 0), :] + g1a[x, y]

    def take_b(x):
        for y in ys:
            to_txt(
                g1b.at[y, x], g1b.at[y, x], b1_send.at[y, x], b1_recv.at[y, x],
                y * minor + mx,
            ).wait_recv()
            gi[block(my, x, 1), :] = gi[block(my, x, 1), :] + g1b[y, x]

    def second_leg():
        for y in ys:
            take_a(y)
            begin([to_txt(
                gi.at[block(y, mx, 0), :], g2a.at[my], a2_send.at[y], a2_recv.at[my],
                y * minor + mx,
            )])
        for x in xs:
            take_b(x)
            begin([to_txt(
                gi.at[block(my, x, 1), :], g2b.at[mx], b2_send.at[x], b2_recv.at[mx],
                my * minor + x,
            )])

    def loss_leg():
        for d, p in enumerate(txt_peers):
            to_txt(lrow.at[p], lrow.at[p], l1_send.at[d], l1_recv.at[p], p).wait_recv()
        lcol[mi] = functools.reduce(jnp.add, [lrow[k] for k in range(txt_n)])
        l2_out = [
            to_img(lcol.at[mi], lcol.at[mi], l2_send.at[d], l2_recv.at[mi], p)
            for d, p in enumerate(img_peers)
        ]
        for copy in l2_out:
            copy.start()
        if levels > 1:
            launch(1)
        return l2_out

    def onward(bp, h, up):
        @pl.when(jnp.logical_and(zp < bp, zp > 0) if up else zp > bp)
        def _():
            at, slot, copy = hop(real(bp), h, 1 - high if up else high)
            copy.wait_recv()
            gt[at, :] = gt[at, :] + slot[...]
            copy.start()

    steps = [
        ((levels - 1 - bp) * 2 + h, True, bp, h) for bp in range(2, levels) for h in range(2)
    ] + [
        (bp * 2 + h + 1.5, False, bp, h) for bp in range(levels // 2) for h in range(2)
    ]
    l2_out = None
    for key, up, bp, h in sorted(steps):
        if key > 1 and l2_out is None:
            second_leg()
            l2_out = loss_leg()
        onward(bp, h, up)
    if l2_out is None:
        second_leg()
        l2_out = loss_leg()

    take_a(my)
    take_b(mx)
    for d, p in enumerate(img_peers):
        to_img(lcol.at[p], lcol.at[p], l2_send.at[d], l2_recv.at[p], p).wait_recv()
    loss_ref[...] = (0.5 * LN2) * functools.reduce(jnp.add, [lcol[k] for k in range(img_n)])

    for way in (0, 1):
        @pl.when(mz > 0 if way else mz < levels - 1)
        def _(way=way):
            for h in range(2):
                at, slot, copy = hop(mz, h, way)
                copy.wait_recv()
                gt[at, :] = gt[at, :] + slot[...]

    gtxt_ref[...] = gt[cols_of(mi), :]
    for y in ys:
        to_txt(
            g2a.at[y], g2a.at[y], a2_send.at[y], a2_recv.at[y], y * minor + mx
        ).wait_recv()
        gi[block(my, mx, 0), :] = gi[block(my, mx, 0), :] + g2a[y]
    for x in xs:
        to_txt(
            g2b.at[x], g2b.at[x], b2_send.at[x], b2_recv.at[x], my * minor + x
        ).wait_recv()
        gi[block(my, mx, 1), :] = gi[block(my, mx, 1), :] + g2b[x]
    gimg_ref[...] = gi[rows_of(mt), :]
    for b in range(levels):
        for way in (0, 1):
            @pl.when(b > mz if way else b < mz)
            def _(b=b, way=way):
                for h in range(2):
                    hop(b, h, way)[2].wait_send()

    for copy in [*stat_out, *gi_out, *x_out, *l1_out, *l2_out]:
        copy.wait_send()


def hand_over(loss, gimg, gtxt, loss_out, gimg_out, gtxt_out):
    loss_out[0, 0] = loss[0, 0]
    gimg_out[...] = gimg[...]
    gtxt_out[...] = gtxt[...]


def body(img_n, txt_n, teacher_img, teacher_txt, student_img, student_txt):
    rows, wide = teacher_img.shape
    cols, deep = student_txt.shape
    levels = img_n // 2
    vmem = pltpu.VMEM
    minor = minor_of(txt_n)
    major = txt_n // minor
    part = rows // txt_n // 2
    dma = pltpu.SemaphoreType.DMA
    bf16 = jnp.bfloat16
    loss, grad_img, grad_txt = pl.pallas_call(
        functools.partial(kernel, img_n, txt_n),
        out_shape=(
            jax.ShapeDtypeStruct((8, LANES), F32),
            jax.ShapeDtypeStruct((rows // txt_n, deep), F32),
            jax.ShapeDtypeStruct((cols // img_n, deep), F32),
        ),
        in_specs=[pl.BlockSpec(memory_space=pltpu.HBM)] * 4,
        out_specs=tuple(pl.BlockSpec(memory_space=vmem) for _ in range(3)),
        scratch_shapes=[
            vmem((rows, wide), bf16), vmem((cols, wide), bf16),
            vmem((rows, deep), bf16), vmem((cols, deep), bf16),
            vmem((rows, cols), F32), vmem((rows, cols), F32), vmem((rows, cols), F32),
            vmem((2, rows, LANES), F32), vmem((2, 8, cols), F32),
            vmem((2, txt_n, 2, rows // LANES, LANES), F32),
            vmem((2, img_n, 2, cols // LANES, LANES), F32),
            vmem((rows, cols), bf16), vmem((cols, rows), bf16),
            vmem((rows, deep), F32), vmem((minor, major, part, deep), F32),
            vmem((major, minor, part, deep), F32),
            vmem((major, part, deep), F32), vmem((minor, part, deep), F32),
            vmem((cols, deep), F32), vmem((levels, cols // img_n, deep), F32),
            vmem((2, levels, cols // img_n, deep), F32),
            vmem((txt_n, 8, LANES), F32), vmem((img_n, 8, LANES), F32),
            dma((4,)),
            dma((2, txt_n)), dma((2, txt_n)), dma((2, img_n)), dma((2, img_n)),
            dma((minor, major)), dma((minor, major)), dma((major, minor)), dma((major, minor)),
            dma((major,)), dma((major,)), dma((minor,)), dma((minor,)), dma((levels,)), dma((levels,)),
            dma((2, levels, 2)), dma((2, levels, 2)),
            dma((txt_n,)), dma((txt_n,)), dma((img_n,)), dma((img_n,)),
        ],
        compiler_params=pltpu.CompilerParams(
            collective_id=0, has_side_effects=True, vmem_limit_bytes=60 * 1024 * 1024
        ),
    )(teacher_img, teacher_txt, student_img, student_txt)
    loss, grad_img, grad_txt = pl.pallas_call(
        hand_over,
        out_shape=(
            jax.ShapeDtypeStruct((1, 1), F32),
            jax.ShapeDtypeStruct(grad_img.shape, F32),
            jax.ShapeDtypeStruct(grad_txt.shape, F32),
        ),
        in_specs=[pl.BlockSpec(memory_space=vmem)] * 3,
        out_specs=(
            pl.BlockSpec(memory_space=pltpu.SMEM),
            pl.BlockSpec(memory_space=vmem), pl.BlockSpec(memory_space=vmem),
        ),
    )(loss, grad_img, grad_txt)
    return loss.reshape(()), grad_img, grad_txt


def solution(mesh):
    placed = (P("img", None), P("txt", None), P("img", None), P("txt", None))
    return jax.shard_map(
        functools.partial(body, mesh.shape["img"], mesh.shape["txt"]),
        mesh=mesh,
        in_specs=placed,
        out_specs=(P(), P(("img", "txt"), None), P(("txt", "img"), None)),
        check_vma=False,
    )
```

time: 57.1 us -> 49.4 us (0.87)
  Pallas kernels: 56.4 us -> 48.6 us
    pallas_call x1, Pallas kernels: 54.3 us -> 46.6 us  [body(): pl.pallas_call(functools.partial(kernel, img_n, txt_n), out_shape=(jax.Sh...]
where the time goes in v1:
time: 49.4 us; the launch traced here: 49.3 us
  Pallas kernels  48.6 us (98%)
  between operations  0.64 us (1%)
    pallas_call x1, Pallas kernels, body(): pl.pallas_call(functools.partial(kernel, img_n, txt_n), out_shape=(jax.Sh...  46.6 us
    pallas_call x1, Pallas kernels, body(): pl.pallas_call(hand_over, out_shape=(jax.ShapeDtypeStruct((1, 1), F32), j...  2.03 us

profile of v1, /device:TPU:0, one launch (start us, length us, event | category | flops | bytes accessed | tf_op | source)
XLA Modules:
  0.0 49.3 jit_solution(3084822381918071387)
XLA Ops:
  0.6 46.6 %shard_map.67 = (f32[8,128]{1,0:T(8,128)}, f32[256,512]{1,0:T(8,128)}, f32[128,512]{1,0:T(8,128)}) custom-call(bf16[1024,1280]{1,0:T(8,128)(2,1)} %timg_hbm.1, bf16[1024,1280]{1,0:T(8,128)(2,1)} %ttxt_hbm.1, bf16[1024,512]{1,0:T(8,128)(2,1)} %simg_hbm.1, bf16[1024,512]{1,0:T(8,128)(2,1)} %stxt_hbm.1), custom_call_target="tpu_custom_call" | custom-call | tf_op jit(solution)/shard_map/pallas_call | solution.py:456
  47.2 2.0 %shard_map.68 = (f32[1,1]{1,0:T(1,128)}, f32[256,512]{1,0:T(8,128)}, f32[128,512]{1,0:T(8,128)}) custom-call(f32[8,128]{1,0:T(8,128)} %get-tuple-element.9.loss, f32[256,512]{1,0:T(8,128)} %get-tuple-element.10.gimg, f32[128,512]{1,0:T(8,128)} %get-tuple-element.11.gtxt), custom_call_target="tpu_custom_call" | custom-call | tf_op jit(solution)/shard_map/pallas_call | solution.py:490

commit v2 on v1

--- a/solution.py
+++ b/solution.py
@@ -24,7 +24,7 @@
     img_n, txt_n,
     timg_hbm, ttxt_hbm, simg_hbm, stxt_hbm,
     loss_ref, gimg_ref, gtxt_ref,
-    timg, ttxt, simg, stxt, t2, s2, q, row_at, cstat, rslot, cslot, delta, deltat,
+    timg, ttxt, simg, stxt, t2, s2, q, row_at, row_sum, cstat, rslot, cslot, delta, deltat,
     gi, g1a, g1b, g2a, g2b, gt, xr, zr, lrow, lcol,
     in_sem, rs_send, rs_recv, cs_send, cs_recv, a1_send, a1_recv, b1_send, b1_recv,
     a2_send, a2_recv, b2_send, b2_recv, x_send, x_recv,
@@ -72,43 +72,35 @@
             device_id=(p, mt), device_id_type=MESH,
         )
 
-    lane = lax.broadcasted_iota(jnp.int32, (8, LANES), 1)
-
     chunk = min(2 * LANES, cols)
+    chunks = cols // chunk
     stat_out = []
 
-    def product(left, right, out, factor, slot):
-        def one(j, c):
-            at = pl.ds(pl.multiple_of(j * chunk, chunk), chunk)
-            tile = factor * lax.dot_general(
-                left[...], right[at, :], NT, preferred_element_type=F32
-            )
-            out[:, at] = tile
-            cstat[slot, 0:1, at] = jnp.max(tile, axis=0, keepdims=True)
-            return c
-
-        lax.fori_loop(0, cols // chunk, one, 0)
-
-    def masses(out, slot):
-        def group(g, mass):
-            here = pl.ds(pl.multiple_of(g * 8, 8), 8)
-            x = out[here, :]
-            peak = jnp.max(x, axis=1, keepdims=True)
-            row = jnp.sum(jnp.exp2(x - peak), axis=1, keepdims=True)
-            row_at[slot, here, :] = jnp.where(lane == 0, peak, row)
-            return mass + jnp.exp2(x - cstat[slot, 0:1, :])
-
-        mass = lax.fori_loop(0, rows // 8, group, jnp.zeros((8, cols), F32), unroll=8)
-        tops = cstat[slot, 0:1, :]
-        sums = jnp.sum(mass, axis=0, keepdims=True)
+    def tile_of(left, right, out, factor, slot, j):
+        at = pl.ds(pl.multiple_of(j * chunk, chunk), chunk)
+        tile = factor * lax.dot_general(
+            left[...], right[at, :], NT, preferred_element_type=F32
+        )
+        out[:, at] = tile
+        cstat[slot, 0:1, at] = jnp.max(tile, axis=0, keepdims=True)
+
+    def lanes(x):
+        return [x[:, k * LANES : (k + 1) * LANES] for k in range(pieces)]
+
+    def group(out, slot, start, mass):
+        here = pl.ds(pl.multiple_of(start, 8), 8)
+        x = out[here, :]
+        peak = functools.reduce(jnp.maximum, lanes(x))
+        row_at[slot, here, :] = peak
+        row_sum[slot, here, :] = functools.reduce(
+            jnp.add, [jnp.exp2(v - peak) for v in lanes(x)]
+        )
+        return mass + jnp.exp2(x - cstat[slot, 0:1, :])
+
+    def share(slot, mass):
+        total = cstat[slot, 0:1, :] + jnp.log(jnp.sum(mass, axis=0, keepdims=True)) * LOG2E
         for k in range(pieces):
-            at = slice(k * LANES, (k + 1) * LANES)
-            cslot[slot, mi, 0, k : k + 1, :] = tops[:, at]
-            cslot[slot, mi, 1, k : k + 1, :] = sums[:, at]
-        for k in range(strips):
-            turned = row_at[slot, k * LANES : (k + 1) * LANES, :].T
-            rslot[slot, mt, 0, k : k + 1, :] = turned[0:1, :]
-            rslot[slot, mt, 1, k : k + 1, :] = turned[1:2, :]
+            cslot[slot, mi, k : k + 1, :] = total[:, k * LANES : (k + 1) * LANES]
         if slot == 1:
             pl.semaphore_wait(barrier, txt_n - 1 + img_n - 1)
         copies = [
@@ -117,7 +109,17 @@
                 cs_send.at[slot, d], cs_recv.at[slot, mi], p,
             )
             for d, p in reversed(list(enumerate(img_peers)))
-        ] + [
+        ]
+        for copy in copies:
+            copy.start()
+        stat_out.extend(copies)
+        for k in range(strips):
+            at = slice(k * LANES, (k + 1) * LANES)
+            peaks = row_at[slot, at, :].T
+            top = jnp.max(peaks, axis=0, keepdims=True)
+            row = jnp.sum(row_sum[slot, at, :].T * jnp.exp2(peaks - top), axis=0, keepdims=True)
+            rslot[slot, mt, k : k + 1, :] = top + jnp.log(row) * LOG2E
+        copies = [
             to_txt(
                 rslot.at[slot, mt], rslot.at[slot, mt],
                 rs_send.at[slot, d], rs_recv.at[slot, mt], p,
@@ -128,21 +130,32 @@
             copy.start()
         stat_out.extend(copies)
 
+    zero = jnp.zeros((8, cols), F32)
     loads[0].wait()
     loads[1].wait()
-    product(simg, stxt, s2, scale_s, 1)
-    masses(s2, 1)
+    lax.fori_loop(
+        0, chunks, lambda j, c: (tile_of(simg, stxt, s2, scale_s, 1, j), c)[1], 0
+    )
     loads[2].wait()
     loads[3].wait()
-    product(timg, ttxt, t2, scale_t, 0)
-    masses(t2, 0)
+
+    share_rows = rows // chunks
+
+    def both(j, mass):
+        tile_of(timg, ttxt, t2, scale_t, 0, j)
+        for g in range(share_rows // 8):
+            mass = group(s2, 1, j * share_rows + g * 8, mass)
+        return mass
+
+    share(1, lax.fori_loop(0, chunks, both, zero))
+    share(0, lax.fori_loop(
+        0, rows // 8, lambda g, mass: group(t2, 0, g * 8, mass), zero, unroll=8
+    ))
 
     def joined(slot, n):
-        peaks = [slot[k, 0] for k in range(n)]
-        top = functools.reduce(jnp.maximum, peaks)
-        mass = functools.reduce(
-            jnp.add, [slot[k, 1] * jnp.exp2(peaks[k] - top) for k in range(n)]
-        )
+        logs = [slot[k] for k in range(n)]
+        top = functools.reduce(jnp.maximum, logs)
+        mass = functools.reduce(jnp.add, [jnp.exp2(v - top) for v in logs])
         return top + jnp.log(mass) * LOG2E
 
     def gathered(slot):
@@ -466,9 +479,9 @@
             vmem((rows, wide), bf16), vmem((cols, wide), bf16),
             vmem((rows, deep), bf16), vmem((cols, deep), bf16),
             vmem((rows, cols), F32), vmem((rows, cols), F32), vmem((rows, cols), F32),
-            vmem((2, rows, LANES), F32), vmem((2, 8, cols), F32),
-            vmem((2, txt_n, 2, rows // LANES, LANES), F32),
-            vmem((2, img_n, 2, cols // LANES, LANES), F32),
+            vmem((2, rows, LANES), F32), vmem((2, rows, LANES), F32), vmem((2, 8, cols), F32),
+            vmem((2, txt_n, rows // LANES, LANES), F32),
+            vmem((2, img_n, cols // LANES, LANES), F32),
             vmem((rows, cols), bf16), vmem((cols, rows), bf16),
             vmem((rows, deep), F32), vmem((minor, major, part, deep), F32),
             vmem((major, minor, part, deep), F32),

time: 49.4 us -> 45.2 us (0.915)
  Pallas kernels: 48.6 us -> 44.4 us
    pallas_call x1, Pallas kernels: 46.6 us -> 42.4 us  [body(): pl.pallas_call(functools.partial(kernel, img_n, txt_n), out_shape=(jax.Sh...]
where the time goes in v2:
time: 45.2 us; the launch traced here: 45.1 us
  Pallas kernels  44.4 us (98%)
  between operations  0.64 us (1%)
    pallas_call x1, Pallas kernels, body(): pl.pallas_call(functools.partial(kernel, img_n, txt_n), out_shape=(jax.Sh...  42.4 us
    pallas_call x1, Pallas kernels, body(): pl.pallas_call(hand_over, out_shape=(jax.ShapeDtypeStruct((1, 1), F32), j...  2.03 us

profile of v2, /device:TPU:0, one launch (start us, length us, event | category | flops | bytes accessed | tf_op | source)
XLA Modules:
  0.0 45.1 jit_solution(13590064117715721791)
XLA Ops:
  0.6 42.4 %shard_map.67 = (f32[8,128]{1,0:T(8,128)}, f32[256,512]{1,0:T(8,128)}, f32[128,512]{1,0:T(8,128)}) custom-call(bf16[1024,1280]{1,0:T(8,128)(2,1)} %timg_hbm.1, bf16[1024,1280]{1,0:T(8,128)(2,1)} %ttxt_hbm.1, bf16[1024,512]{1,0:T(8,128)(2,1)} %simg_hbm.1, bf16[1024,512]{1,0:T(8,128)(2,1)} %stxt_hbm.1), custom_call_target="tpu_custom_call" | custom-call | tf_op jit(solution)/shard_map/pallas_call | solution.py:469
  43.0 2.0 %shard_map.68 = (f32[1,1]{1,0:T(1,128)}, f32[256,512]{1,0:T(8,128)}, f32[128,512]{1,0:T(8,128)}) custom-call(f32[8,128]{1,0:T(8,128)} %get-tuple-element.9.loss, f32[256,512]{1,0:T(8,128)} %get-tuple-element.10.gimg, f32[128,512]{1,0:T(8,128)} %get-tuple-element.11.gtxt), custom_call_target="tpu_custom_call" | custom-call | tf_op jit(solution)/shard_map/pallas_call | solution.py:503

commit v3 on v2

--- a/solution.py
+++ b/solution.py
@@ -76,8 +76,7 @@
     chunks = cols // chunk
     stat_out = []
 
-    def tile_of(left, right, out, factor, slot, j):
-        at = pl.ds(pl.multiple_of(j * chunk, chunk), chunk)
+    def tile_of(left, right, out, factor, slot, at):
         tile = factor * lax.dot_general(
             left[...], right[at, :], NT, preferred_element_type=F32
         )
@@ -87,7 +86,7 @@
     def lanes(x):
         return [x[:, k * LANES : (k + 1) * LANES] for k in range(pieces)]
 
-    def group(out, slot, start, mass):
+    def row_group(out, slot, start):
         here = pl.ds(pl.multiple_of(start, 8), 8)
         x = out[here, :]
         peak = functools.reduce(jnp.maximum, lanes(x))
@@ -95,14 +94,15 @@
         row_sum[slot, here, :] = functools.reduce(
             jnp.add, [jnp.exp2(v - peak) for v in lanes(x)]
         )
-        return mass + jnp.exp2(x - cstat[slot, 0:1, :])
-
-    def share(slot, mass):
-        total = cstat[slot, 0:1, :] + jnp.log(jnp.sum(mass, axis=0, keepdims=True)) * LOG2E
-        for k in range(pieces):
-            cslot[slot, mi, k : k + 1, :] = total[:, k * LANES : (k + 1) * LANES]
-        if slot == 1:
-            pl.semaphore_wait(barrier, txt_n - 1 + img_n - 1)
+        return x
+
+    def col_log(slot, at, mass):
+        total = cstat[slot, 0:1, at] + jnp.log(jnp.sum(mass, axis=0, keepdims=True)) * LOG2E
+        for k in range(at.start // LANES, at.stop // LANES):
+            here = slice(k * LANES - at.start, (k + 1) * LANES - at.start)
+            cslot[slot, mi, k : k + 1, :] = total[:, here]
+
+    def send_cols(slot):
         copies = [
             to_img(
                 cslot.at[slot, mi], cslot.at[slot, mi],
@@ -113,6 +113,8 @@
         for copy in copies:
             copy.start()
         stat_out.extend(copies)
+
+    def send_rows(slot):
         for k in range(strips):
             at = slice(k * LANES, (k + 1) * LANES)
             peaks = row_at[slot, at, :].T
@@ -130,27 +132,41 @@
             copy.start()
         stat_out.extend(copies)
 
-    zero = jnp.zeros((8, cols), F32)
+    tiles = [slice(j * chunk, (j + 1) * chunk) for j in range(chunks)]
     loads[0].wait()
     loads[1].wait()
-    lax.fori_loop(
-        0, chunks, lambda j, c: (tile_of(simg, stxt, s2, scale_s, 1, j), c)[1], 0
-    )
+    lax.fori_loop(0, chunks, lambda j, c: (tile_of(
+        simg, stxt, s2, scale_s, 1, pl.ds(pl.multiple_of(j * chunk, chunk), chunk)
+    ), c)[1], 0)
     loads[2].wait()
     loads[3].wait()
 
-    share_rows = rows // chunks
-
-    def both(j, mass):
-        tile_of(timg, ttxt, t2, scale_t, 0, j)
-        for g in range(share_rows // 8):
-            mass = group(s2, 1, j * share_rows + g * 8, mass)
-        return mass
-
-    share(1, lax.fori_loop(0, chunks, both, zero))
-    share(0, lax.fori_loop(
-        0, rows // 8, lambda g, mass: group(t2, 0, g * 8, mass), zero, unroll=8
-    ))
+    def col_mass(at):
+        mass = jnp.zeros((8, chunk), F32)
+        for g in range(rows // 8):
+            mass = mass + jnp.exp2(t2[g * 8 : g * 8 + 8, at] - cstat[0, 0:1, at])
+        col_log(0, at, mass)
+
+    early = max(1, chunks // 2)
+    share_rows = rows // early
+    mass = jnp.zeros((8, cols), F32)
+    for j, at in enumerate(tiles):
+        if j == early:
+            col_log(1, slice(0, cols), mass)
+            pl.semaphore_wait(barrier, txt_n - 1 + img_n - 1)
+            send_cols(1)
+            send_rows(1)
+        if j > 0:
+            col_mass(tiles[j - 1])
+        tile_of(timg, ttxt, t2, scale_t, 0, at)
+        if j < early:
+            for g in range(share_rows // 8):
+                x = row_group(s2, 1, j * share_rows + g * 8)
+                mass = mass + jnp.exp2(x - cstat[1, 0:1, :])
+    col_mass(tiles[-1])
+    send_cols(0)
+    lax.fori_loop(0, rows // 8, lambda g, c: (row_group(t2, 0, g * 8), c)[1], 0, unroll=8)
+    send_rows(0)
 
     def joined(slot, n):
         logs = [slot[k] for k in range(n)]
@@ -190,7 +206,7 @@
         q[here, :] = jnp.exp2(sg - spread(1, here)) + jnp.exp2(sg - cstat[1, 0:1, :])
         return c
 
-    lax.fori_loop(0, rows // 8, student_group, 0, unroll=8)
+    lax.fori_loop(0, rows // 8, student_group, 0, unroll=4)
     row_t, col_t = gathered(0)
 
     per = rows // txt_n
@@ -210,24 +226,26 @@
     def cols_of(o):
         return pl.ds(pl.multiple_of(o * cper, cper), cper)
 
+    def delta_tiles(row_starts, b):
+        for r0 in row_starts:
+            at = pl.ds(pl.multiple_of(r0, LANES), LANES)
+            r = row_at[0, at, :]
+            for n in range(wide_c // LANES):
+                cs = pl.ds(pl.multiple_of(b * wide_c + n * LANES, LANES), LANES)
+                tg = t2[at, cs]
+                d = q[at, cs] - jnp.exp2(tg - r) - jnp.exp2(tg - cstat[0, 0:1, cs])
+                d = (8.0 * d).astype(jnp.bfloat16)
+                delta[at, cs] = d
+                deltat[cs, at] = d.T
+
     def delta_block(b):
-        first = pl.multiple_of(b * wide_c, LANES)
         group = 4 if strips % 4 == 0 else 1
-
-        def some(g, c):
-            for k in range(group):
-                at = pl.ds(pl.multiple_of((g * group + k) * LANES, LANES), LANES)
-                r = row_at[0, at, :]
-                for n in range(wide_c // LANES):
-                    cs = pl.ds(pl.multiple_of(first + n * LANES, LANES), LANES)
-                    tg = t2[at, cs]
-                    d = q[at, cs] - jnp.exp2(tg - r) - jnp.exp2(tg - cstat[0, 0:1, cs])
-                    d = (8.0 * d).astype(jnp.bfloat16)
-                    delta[at, cs] = d
-                    deltat[cs, at] = d.T
-            return c
-
-        lax.fori_loop(0, strips // group, some, 0)
+        lax.fori_loop(
+            0, strips // group,
+            lambda g, c: (
+                delta_tiles([(g * group + k) * LANES for k in range(group)], b), c
+            )[1], 0,
+        )
 
     x_out = []
 
@@ -260,15 +278,6 @@
             for h in range(2):
                 hop(real(bp), h, 1 - high)[2].start()
 
-    far = list(reversed(range(levels)))
-    lag = 2
-    for n, bp in enumerate(far):
-        delta_block(real(bp))
-        text_pair(real(bp))
-        if n >= lag:
-            merge_mate(real(far[n - lag]))
-            launch(far[n - lag])
-
     gi_out = []
     minor = minor_of(txt_n)
     major = txt_n // minor
@@ -304,19 +313,45 @@
             b1_send.at[y, x], b1_recv.at[my, x], y * minor + mx,
         )
 
-    for y in ys:
-        for x in xs:
+    far = list(reversed(range(levels)))
+    diag = [(y, x) for y in ys for x in xs]
+    side = [(y, mx) for y in ys] + [(my, x) for x in xs] + [(my, mx)]
+    lag = min(2, levels)
+    fine = per % LANES == 0
+
+    def strips_of(blocks):
+        return [
+            (y * minor + x) * per + k * LANES for y, x in blocks for k in range(per // LANES)
+        ]
+
+    def images():
+        for y, x in diag:
             image_term(y, x)
             begin([image_a(y, x), image_b(y, x)])
+
+    for bp in far[:lag]:
+        delta_block(real(bp))
+        text_pair(real(bp))
+    if fine:
+        for bp in far[lag:]:
+            delta_tiles(strips_of(diag), real(bp))
+        images()
+    for n, bp in enumerate(far[lag:]):
+        merge_mate(real(far[n]))
+        launch(far[n])
+        if fine:
+            delta_tiles(strips_of(side), real(bp))
+        else:
+            delta_block(real(bp))
+        text_pair(real(bp))
+    if not fine:
+        images()
     for bp in far[max(0, levels - lag) :]:
         merge_mate(real(bp))
         if bp > 1:
             launch(bp)
-    for y in ys:
-        image_term(y, mx)
-    for x in xs:
-        image_term(my, x)
-    image_term(my, mx)
+    for y, x in side:
+        image_term(y, x)
 
     def teacher_group(g, acc):
         here = pl.ds(pl.multiple_of(g * 8, 8), 8)
@@ -450,10 +485,16 @@
         copy.wait_send()
 
 
-def hand_over(loss, gimg, gtxt, loss_out, gimg_out, gtxt_out):
+def hand_over(loss, gimg, gtxt, loss_out, gimg_out, gtxt_out, sem):
+    copies = [
+        pltpu.make_async_copy(gimg, gimg_out, sem.at[0]),
+        pltpu.make_async_copy(gtxt, gtxt_out, sem.at[1]),
+    ]
+    for copy in copies:
+        copy.start()
     loss_out[0, 0] = loss[0, 0]
-    gimg_out[...] = gimg[...]
-    gtxt_out[...] = gtxt[...]
+    for copy in copies:
+        copy.wait()
 
 
 def body(img_n, txt_n, teacher_img, teacher_txt, student_img, student_txt):
@@ -497,9 +538,9 @@
             dma((txt_n,)), dma((txt_n,)), dma((img_n,)), dma((img_n,)),
         ],
         compiler_params=pltpu.CompilerParams(
-            collective_id=0, has_side_effects=True, vmem_limit_bytes=60 * 1024 * 1024
+            collective_id=0, has_side_effects=True, vmem_limit_bytes=48 * 1024 * 1024
         ),
-    )(teacher_img, teacher_txt, student_img, student_txt)
+    )(*[pltpu.with_memory_space_constraint(v, pltpu.HBM) for v in (teacher_img, teacher_txt, student_img, student_txt)])
     loss, grad_img, grad_txt = pl.pallas_call(
         hand_over,
         out_shape=(
@@ -510,8 +551,10 @@
         in_specs=[pl.BlockSpec(memory_space=vmem)] * 3,
         out_specs=(
             pl.BlockSpec(memory_space=pltpu.SMEM),
-            pl.BlockSpec(memory_space=vmem), pl.BlockSpec(memory_space=vmem),
+            pl.BlockSpec(memory_space=pltpu.HBM), pl.BlockSpec(memory_space=pltpu.HBM),
         ),
+        scratch_shapes=[dma((2,))],
+        compiler_params=pltpu.CompilerParams(vmem_limit_bytes=1024 * 1024),
     )(loss, grad_img, grad_txt)
     return loss.reshape(()), grad_img, grad_txt
 

time: 45.2 us -> 41.2 us (0.912)
  Pallas kernels: 44.4 us -> 40.4 us
    pallas_call x1, Pallas kernels: 42.4 us -> 39 us  [body(): pl.pallas_call(functools.partial(kernel, img_n, txt_n), out_shape=(jax.Sh...]
    pallas_call x1, Pallas kernels: 2.03 us -> 1.41 us  [body(): pl.pallas_call(hand_over, out_shape=(jax.ShapeDtypeStruct((1, 1), F32), j...]
where the time goes in v3:
time: 41.2 us; the launch traced here: 41.1 us
  Pallas kernels  40.4 us (98%)
  between operations  0.64 us (2%)
    pallas_call x1, Pallas kernels, body(): pl.pallas_call(functools.partial(kernel, img_n, txt_n), out_shape=(jax.Sh...  39 us
    pallas_call x1, Pallas kernels, body(): pl.pallas_call(hand_over, out_shape=(jax.ShapeDtypeStruct((1, 1), F32), j...  1.41 us

profile of v3, /device:TPU:0, one launch (start us, length us, event | category | flops | bytes accessed | tf_op | source)
XLA Modules:
  0.0 41.1 jit_solution(11184204538261571304)
XLA Ops:
  0.6 39.0 %shard_map.67 = (f32[8,128]{1,0:T(8,128)S(1)}, f32[256,512]{1,0:T(8,128)S(1)}, f32[128,512]{1,0:T(8,128)S(1)}) custom-call(bf16[1024,1280]{1,0:T(8,128)(2,1)} %timg_hbm.1, bf16[1024,1280]{1,0:T(8,128)(2,1)} %ttxt_hbm.1, bf16[1024,512]{1,0:T(8,128)(2,1)} %simg_hbm.1, bf16[1024,512]{1,0:T(8,128)(2,1)} %stxt_hbm.1), custom_call_target="tpu_custom_call" | custom-call | tf_op jit(solution)/shard_map/pallas_call | solution.py:510
  39.6 1.4 %shard_map.68 = (f32[1,1]{1,0:T(1,128)}, f32[256,512]{1,0:T(8,128)}, f32[128,512]{1,0:T(8,128)}) custom-call(f32[8,128]{1,0:T(8,128)S(1)} %get-tuple-element.9.loss, f32[256,512]{1,0:T(8,128)S(1)} %get-tuple-element.10.gimg, f32[128,512]{1,0:T(8,128)S(1)} %get-tuple-element.11.gtxt), custom_call_target="tpu_custom_call" | custom-call | tf_op jit(solution)/shard_map/pallas_call | solution.py:544

commit v4 on v3

--- a/solution.py
+++ b/solution.py
@@ -226,34 +226,44 @@
     def cols_of(o):
         return pl.ds(pl.multiple_of(o * cper, cper), cper)
 
-    def delta_tiles(row_starts, b):
-        for r0 in row_starts:
-            at = pl.ds(pl.multiple_of(r0, LANES), LANES)
-            r = row_at[0, at, :]
-            for n in range(wide_c // LANES):
-                cs = pl.ds(pl.multiple_of(b * wide_c + n * LANES, LANES), LANES)
-                tg = t2[at, cs]
-                d = q[at, cs] - jnp.exp2(tg - r) - jnp.exp2(tg - cstat[0, 0:1, cs])
-                d = (8.0 * d).astype(jnp.bfloat16)
-                delta[at, cs] = d
-                deltat[cs, at] = d.T
-
-    def delta_block(b):
-        group = 4 if strips % 4 == 0 else 1
-        lax.fori_loop(
-            0, strips // group,
-            lambda g, c: (
-                delta_tiles([(g * group + k) * LANES for k in range(group)], b), c
-            )[1], 0,
-        )
+    def delta_tile(r0, b, n, keep):
+        at = pl.ds(pl.multiple_of(r0, LANES), LANES)
+        for k in range(wide_c // LANES):
+            cs = pl.ds(pl.multiple_of(b * wide_c + k * LANES, LANES), LANES)
+            tg = t2[at, cs]
+            d = q[at, cs] - jnp.exp2(tg - row_at[0, at, :]) - jnp.exp2(tg - cstat[0, 0:1, cs])
+            d = (8.0 * d).astype(jnp.bfloat16)
+            keep(cs, d)
+            deltat[n, k * LANES : (k + 1) * LANES, at] = d.T
+
+    def delta_blocks(found, b, n):
+        for slot, (y, x) in found:
+            for k in range(per // LANES):
+                def keep(cs, d, slot=slot, k=k):
+                    delta[slot, k * LANES : (k + 1) * LANES, cs] = d
+
+                delta_tile((y * minor + x) * per + k * LANES, b, n, keep)
+
+    def delta_strips(b, n):
+        def one(g, c):
+            def keep(cs, d):
+                for k in range(LANES // per):
+                    delta[g * (LANES // per) + k, :, cs] = d[k * per : (k + 1) * per]
+
+            delta_tile(g * LANES, b, n, keep)
+            return c
+
+        lax.fori_loop(0, strips, one, 0)
 
     x_out = []
 
-    def text_pair(b):
+    def text_pair(b, n):
         pair = pl.ds(pl.multiple_of(b * wide_c, wide_c), wide_c)
         gt[pair, :] = scale_g * jnp.dot(
-            deltat[pair, :], simg[...], preferred_element_type=F32
-        )
+            deltat[n], simg[...], preferred_element_type=F32
+        )
+
+    def text_mate(b):
         o = 2 * b + 1 - mc
         copy = to_img(gt.at[cols_of(o), :], xr.at[b], x_send.at[b], x_recv.at[b], mate)
         copy.start()
@@ -290,10 +300,9 @@
     ys = [lax.rem(my + d, major) for d in range(1, major)]
     xs = [lax.rem(mx + d, minor) for d in range(1, minor)]
 
-    def image_term(y, x):
-        p = y * minor + x
-        gi[rows_of(p), :] = scale_g * jnp.dot(
-            delta[rows_of(p), :], stxt[...], preferred_element_type=F32
+    def image_term(y, x, slot):
+        gi[rows_of(y * minor + x), :] = scale_g * jnp.dot(
+            delta[slot], stxt[...], preferred_element_type=F32
         )
 
     def begin(copies):
@@ -316,42 +325,58 @@
     far = list(reversed(range(levels)))
     diag = [(y, x) for y in ys for x in xs]
     side = [(y, mx) for y in ys] + [(my, x) for x in xs] + [(my, mx)]
-    lag = min(2, levels)
+    blocks = list(enumerate(diag + side))
     fine = per % LANES == 0
 
-    def strips_of(blocks):
-        return [
-            (y * minor + x) * per + k * LANES for y, x in blocks for k in range(per // LANES)
-        ]
-
-    def images():
+    def images(found):
+        for slot, (y, x) in found:
+            image_term(y, x, slot if fine else y * minor + x)
+
+    def first_images():
         for y, x in diag:
-            image_term(y, x)
             begin([image_a(y, x), image_b(y, x)])
 
-    for bp in far[:lag]:
-        delta_block(real(bp))
-        text_pair(real(bp))
-    if fine:
-        for bp in far[lag:]:
-            delta_tiles(strips_of(diag), real(bp))
-        images()
-    for n, bp in enumerate(far[lag:]):
-        merge_mate(real(far[n]))
-        launch(far[n])
-        if fine:
-            delta_tiles(strips_of(side), real(bp))
-        else:
-            delta_block(real(bp))
-        text_pair(real(bp))
-    if not fine:
-        images()
-    for bp in far[max(0, levels - lag) :]:
+    def pass_on(bp):
         merge_mate(real(bp))
         if bp > 1:
             launch(bp)
-    for y, x in side:
-        image_term(y, x)
+
+    if fine:
+        corner, rest = blocks[: len(diag)], blocks[len(diag) :]
+        delta_blocks(blocks, real(far[0]), 0)
+        text_pair(real(far[0]), 0)
+        text_mate(real(far[0]))
+        for n, bp in enumerate(far[1:]):
+            delta_blocks(corner, real(bp), n + 1)
+        if levels > 1:
+            delta_blocks(rest, real(far[1]), 1)
+        images(corner)
+        first_images()
+        if levels > 2:
+            pass_on(far[0])
+        for n in range(1, levels):
+            if n + 1 < levels:
+                delta_blocks(rest, real(far[n + 1]), n + 1)
+            text_pair(real(far[n]), n)
+            text_mate(real(far[n]))
+            if n > 2:
+                pass_on(far[n - 2])
+        images(rest[:1])
+        for bp in far[max(0, levels - 2) :]:
+            pass_on(bp)
+        images(rest[1:])
+    else:
+        for n, bp in enumerate(far):
+            delta_strips(real(bp), n)
+            text_pair(real(bp), n)
+            text_mate(real(bp))
+            if n > 1:
+                pass_on(far[n - 2])
+        images(blocks[: len(diag)])
+        first_images()
+        for bp in far[max(0, levels - 2) :]:
+            pass_on(bp)
+        images(blocks[len(diag) :])
 
     def teacher_group(g, acc):
         here = pl.ds(pl.multiple_of(g * 8, 8), 8)
@@ -363,7 +388,7 @@
             p_row * (1.0 / (rows * img_n)) + p_col * (1.0 / (cols * txt_n))
         ) * gap
 
-    total = lax.fori_loop(0, rows // 8, teacher_group, jnp.zeros((8, cols), F32), unroll=4)
+    total = lax.fori_loop(0, rows // 8, teacher_group, jnp.zeros((8, cols), F32), unroll=8)
     mine = (
         jnp.sum(total)
         + jnp.sum(row_s - row_t) * (1.0 / (rows * img_n * txt_n))
@@ -523,7 +548,7 @@
             vmem((2, rows, LANES), F32), vmem((2, rows, LANES), F32), vmem((2, 8, cols), F32),
             vmem((2, txt_n, rows // LANES, LANES), F32),
             vmem((2, img_n, cols // LANES, LANES), F32),
-            vmem((rows, cols), bf16), vmem((cols, rows), bf16),
+            vmem((txt_n, rows // txt_n, cols), bf16), vmem((levels, cols // levels, rows), bf16),
             vmem((rows, deep), F32), vmem((minor, major, part, deep), F32),
             vmem((major, minor, part, deep), F32),
             vmem((major, part, deep), F32), vmem((minor, part, deep), F32),

time: 41.2 us -> 40.8 us (level)
  no operation moved by 1% of the time
where the time goes in v4:
time: 40.8 us; the launch traced here: 40.7 us
  Pallas kernels  40 us (98%)
  between operations  0.64 us (2%)
    pallas_call x1, Pallas kernels, body(): pl.pallas_call(functools.partial(kernel, img_n, txt_n), out_shape=(jax.Sh...  38.6 us
    pallas_call x1, Pallas kernels, body(): pl.pallas_call(hand_over, out_shape=(jax.ShapeDtypeStruct((1, 1), F32), j...  1.41 us

profile of v4, /device:TPU:0, one launch (start us, length us, event | category | flops | bytes accessed | tf_op | source)
XLA Modules:
  0.0 40.7 jit_solution(17571874017554290497)
XLA Ops:
  0.6 38.6 %shard_map.67 = (f32[8,128]{1,0:T(8,128)S(1)}, f32[256,512]{1,0:T(8,128)S(1)}, f32[128,512]{1,0:T(8,128)S(1)}) custom-call(bf16[1024,1280]{1,0:T(8,128)(2,1)} %timg_hbm.1, bf16[1024,1280]{1,0:T(8,128)(2,1)} %ttxt_hbm.1, bf16[1024,512]{1,0:T(8,128)(2,1)} %simg_hbm.1, bf16[1024,512]{1,0:T(8,128)(2,1)} %stxt_hbm.1), custom_call_target="tpu_custom_call" | custom-call | tf_op jit(solution)/shard_map/pallas_call | solution.py:535
  39.3 1.4 %shard_map.68 = (f32[1,1]{1,0:T(1,128)}, f32[256,512]{1,0:T(8,128)}, f32[128,512]{1,0:T(8,128)}) custom-call(f32[8,128]{1,0:T(8,128)S(1)} %get-tuple-element.9.loss, f32[256,512]{1,0:T(8,128)S(1)} %get-tuple-element.10.gimg, f32[128,512]{1,0:T(8,128)S(1)} %get-tuple-element.11.gtxt), custom_call_target="tpu_custom_call" | custom-call | tf_op jit(solution)/shard_map/pallas_call | solution.py:569

commit v5 on v4

--- a/solution.py
+++ b/solution.py
@@ -54,7 +54,8 @@
 
     barrier = pltpu.get_barrier_semaphore()
     txt_peers = [lax.rem(mt + d, txt_n) for d in range(1, txt_n)]
-    img_peers = [lax.rem(mi + d, img_n) for d in range(1, img_n)]
+    step = 1 + (1 - (2 * mz) // levels) * (img_n - 2)
+    img_peers = [lax.rem(mi + d * step, img_n) for d in range(1, img_n)]
     for p in txt_peers:
         pl.semaphore_signal(barrier, inc=1, device_id=(mi, p), device_id_type=MESH)
     for p in img_peers:
@@ -108,7 +109,7 @@
                 cslot.at[slot, mi], cslot.at[slot, mi],
                 cs_send.at[slot, d], cs_recv.at[slot, mi], p,
             )
-            for d, p in reversed(list(enumerate(img_peers)))
+            for d, p in enumerate(img_peers)
         ]
         for copy in copies:
             copy.start()
@@ -135,9 +136,8 @@
     tiles = [slice(j * chunk, (j + 1) * chunk) for j in range(chunks)]
     loads[0].wait()
     loads[1].wait()
-    lax.fori_loop(0, chunks, lambda j, c: (tile_of(
-        simg, stxt, s2, scale_s, 1, pl.ds(pl.multiple_of(j * chunk, chunk), chunk)
-    ), c)[1], 0)
+    for at in tiles:
+        tile_of(simg, stxt, s2, scale_s, 1, at)
     loads[2].wait()
     loads[3].wait()
 
@@ -488,17 +488,17 @@
                 gt[at, :] = gt[at, :] + slot[...]
 
     gtxt_ref[...] = gt[cols_of(mi), :]
+    gimg_ref[...] = gi[rows_of(mt), :]
     for y in ys:
         to_txt(
             g2a.at[y], g2a.at[y], a2_send.at[y], a2_recv.at[y], y * minor + mx
         ).wait_recv()
-        gi[block(my, mx, 0), :] = gi[block(my, mx, 0), :] + g2a[y]
+        gimg_ref[0:part, :] = gimg_ref[0:part, :] + g2a[y]
     for x in xs:
         to_txt(
             g2b.at[x], g2b.at[x], b2_send.at[x], b2_recv.at[x], my * minor + x
         ).wait_recv()
-        gi[block(my, mx, 1), :] = gi[block(my, mx, 1), :] + g2b[x]
-    gimg_ref[...] = gi[rows_of(mt), :]
+        gimg_ref[part:per, :] = gimg_ref[part:per, :] + g2b[x]
     for b in range(levels):
         for way in (0, 1):
             @pl.when(b > mz if way else b < mz)

time: 40.8 us -> 40.4 us (level)
    pallas_call x1, Pallas kernels: 38.6 us -> 38.2 us  [body(): pl.pallas_call(functools.partial(kernel, img_n, txt_n), out_shape=(jax.Sh...]
where the time goes in v5:
time: 40.4 us; the launch traced here: 40.3 us
  Pallas kernels  39.6 us (98%)
  between operations  0.64 us (2%)
    pallas_call x1, Pallas kernels, body(): pl.pallas_call(functools.partial(kernel, img_n, txt_n), out_shape=(jax.Sh...  38.2 us
    pallas_call x1, Pallas kernels, body(): pl.pallas_call(hand_over, out_shape=(jax.ShapeDtypeStruct((1, 1), F32), j...  1.41 us

profile of v5, /device:TPU:0, one launch (start us, length us, event | category | flops | bytes accessed | tf_op | source)
XLA Modules:
  0.0 40.3 jit_solution(4581909875371923574)
XLA Ops:
  0.6 38.2 %shard_map.67 = (f32[8,128]{1,0:T(8,128)S(1)}, f32[256,512]{1,0:T(8,128)S(1)}, f32[128,512]{1,0:T(8,128)S(1)}) custom-call(bf16[1024,1280]{1,0:T(8,128)(2,1)} %timg_hbm.1, bf16[1024,1280]{1,0:T(8,128)(2,1)} %ttxt_hbm.1, bf16[1024,512]{1,0:T(8,128)(2,1)} %simg_hbm.1, bf16[1024,512]{1,0:T(8,128)(2,1)} %stxt_hbm.1), custom_call_target="tpu_custom_call" | custom-call | tf_op jit(solution)/shard_map/pallas_call | solution.py:535
  38.8 1.4 %shard_map.68 = (f32[1,1]{1,0:T(1,128)}, f32[256,512]{1,0:T(8,128)}, f32[128,512]{1,0:T(8,128)}) custom-call(f32[8,128]{1,0:T(8,128)S(1)} %get-tuple-element.9.loss, f32[256,512]{1,0:T(8,128)S(1)} %get-tuple-element.10.gimg, f32[128,512]{1,0:T(8,128)S(1)} %get-tuple-element.11.gtxt), custom_call_target="tpu_custom_call" | custom-call | tf_op jit(solution)/shard_map/pallas_call | solution.py:569
